TPU v7x, 32 devices: a whole 2x2x4 slice. The times are simulated.
32 devices in a mesh: grp: 8 (over z, y), mem: 4 (over x, core).
Axes of the slice: x: 2, y: 2, z: 4, core: 2. Of those that a mesh axis runs over, the one named last changes fastest.
Arguments:
- client_input: bfloat16 [8, 4, 128, 896], P('grp', 'mem'), may hold values from -6 to 6
- client_gain: float32 [4, 896], P('mem'), may hold values from 0.5 to 1.5
- w_query: bfloat16 [4, 896, 896], P('mem'), may hold values from -1.5 to 1.5
- w_keyval: bfloat16 [4, 896, 256], P('mem'), may hold values from -0.5 to 0.5
- w_out: bfloat16 [4, 896, 896], P('mem'), may hold values from -0.1875 to 0.1875
- server_gain: float32 [8, 896], P('grp'), may hold values from 0.5 to 1.5
- w_gate: bfloat16 [8, 896, 4864], P('grp', None, 'mem'), may hold values from -0.1875 to 0.1875
- w_up: bfloat16 [8, 896, 4864], P('grp', None, 'mem'), may hold values from -0.1875 to 0.1875
- w_down: bfloat16 [8, 4864, 896], P('grp', 'mem'), may hold values from -0.078125 to 0.078125
- out_grad: bfloat16 [8, 4, 128, 896], P('grp', 'mem'), may hold values from -6 to 6
- valid: int32 [8, 4], P('grp', 'mem'), may hold values from 64 to 128
Outputs:
- server_out: bfloat16 [8, 4, 128, 896], P('grp', 'mem')
- grad_query: bfloat16 [4, 896, 896], P('mem')
- grad_keyval: bfloat16 [4, 896, 256], P('mem')
- grad_out: bfloat16 [4, 896, 896], P('mem')
- grad_gate: bfloat16 [8, 896, 4864], P('grp', None, 'mem')
- grad_up: bfloat16 [8, 896, 4864], P('grp', None, 'mem')
- grad_down: bfloat16 [8, 4864, 896], P('grp', 'mem')
All inputs are finite; a program needn't handle non-finite values.
Results may differ from a plain program's by a relative error of at most 0.03.
Values may be sent and summed in bfloat16 or wider, within the bound.
A program may use at most 128 MiB of HBM per device.

v0:
```python
import jax
import jax.numpy as jnp
from jax import lax
from jax.sharding import PartitionSpec as P

KV_HEADS = 2
HEAD_DIM = 64
EPS = 1e-06


def client_forward(tokens_in, gain_vec, query_w, keyval_w, output_w):
    x_float = tokens_in.astype(jnp.float32)
    inv_rms = lax.rsqrt(jnp.mean(x_float * x_float, axis=-1, keepdims=True) + EPS)
    normed = (x_float * inv_rms * gain_vec).astype(jnp.bfloat16)
    queries = jnp.dot(normed, query_w, preferred_element_type=jnp.float32).astype(jnp.bfloat16)
    key_vals = jnp.dot(normed, keyval_w, preferred_element_type=jnp.float32).astype(jnp.bfloat16)
    length = tokens_in.shape[0]
    half_cols = KV_HEADS * HEAD_DIM
    q_heads = queries.reshape(length, KV_HEADS, -1, HEAD_DIM)
    k_heads = key_vals[:, :half_cols].reshape(length, KV_HEADS, HEAD_DIM)
    v_heads = key_vals[:, half_cols:].reshape(length, KV_HEADS, HEAD_DIM)
    scores = jnp.einsum(
        "tgqd,sgd->gqts", q_heads, k_heads, preferred_element_type=jnp.float32
    ) * HEAD_DIM ** (-0.5)
    causal = jnp.arange(length)[:, None] >= jnp.arange(length)[None, :]
    scores = jnp.where(causal, scores, -1e30)
    highest = jnp.max(scores, axis=-1, keepdims=True)
    expo = jnp.exp(scores - highest)
    probs = (expo / jnp.sum(expo, axis=-1, keepdims=True)).astype(jnp.bfloat16)
    attended = jnp.einsum("gqts,sgd->tgqd", probs, v_heads, preferred_element_type=jnp.float32)
    attended = attended.astype(jnp.bfloat16).reshape(length, -1)
    mixed = jnp.dot(attended, output_w, preferred_element_type=jnp.float32)
    return (x_float + mixed).astype(jnp.bfloat16)


def norm_back(h_float, inv_rms, gain_vec, upstream):
    scaled = upstream * gain_vec
    return inv_rms * scaled - h_float * inv_rms**3 * jnp.mean(
        scaled * h_float, axis=-1, keepdims=True
    )


def on_device(
    client_input,
    client_gain,
    w_query,
    w_keyval,
    w_out,
    server_gain,
    w_gate,
    w_up,
    w_down,
    out_grad,
    valid,
):
    tokens_in = client_input[0, 0]
    gain_vec = client_gain[0]
    query_w = w_query[0]
    keyval_w = w_keyval[0]
    output_w = w_out[0]
    s_gain = server_gain[0]
    gate_w = w_gate[0]
    up_w = w_up[0]
    down_w = w_down[0]
    length = tokens_in.shape[0]
    width = tokens_in.shape[1]
    contract_last = (((1,), (1,)), ((), ()))
    contract_first = (((0,), (0,)), ((), ()))

    def client_part(query_in, keyval_in, output_in):
        return client_forward(tokens_in, gain_vec, query_in, keyval_in, output_in)

    own_cut, pull = jax.vjp(client_part, query_w, keyval_w, output_w)
    live = jnp.arange(length) < valid[0, 0]
    own_cot = jnp.where(live[:, None], out_grad[0, 0], jnp.zeros_like(out_grad[0, 0]))
    all_cut = lax.all_gather(own_cut, "mem", axis=0, tiled=True)
    all_cot = lax.all_gather(own_cot, "mem", axis=0, tiled=True)
    h_float = all_cut.astype(jnp.float32)
    inv_rms = lax.rsqrt(jnp.mean(h_float * h_float, axis=-1, keepdims=True) + EPS)
    normed = (h_float * inv_rms * s_gain).astype(jnp.bfloat16)
    gate_act = jnp.dot(normed, gate_w, preferred_element_type=jnp.float32)
    up_act = jnp.dot(normed, up_w, preferred_element_type=jnp.float32)
    sigma = jax.nn.sigmoid(gate_act)
    hidden = (gate_act * sigma * up_act).astype(jnp.bfloat16)
    served = lax.psum_scatter(
        jnp.dot(hidden, down_w, preferred_element_type=jnp.float32).astype(jnp.bfloat16),
        "mem",
        scatter_dimension=0,
        tiled=True,
    ).astype(jnp.float32)
    own_float = own_cut.astype(jnp.float32)
    server_out = (own_float + served).astype(jnp.bfloat16)
    d_hidden = lax.dot_general(all_cot, down_w, contract_last, preferred_element_type=jnp.float32)
    d_gate = (d_hidden * up_act * sigma * (1.0 + gate_act * (1.0 - sigma))).astype(jnp.bfloat16)
    d_up = (d_hidden * gate_act * sigma).astype(jnp.bfloat16)
    grad_down = lax.dot_general(
        hidden, all_cot, contract_first, preferred_element_type=jnp.float32
    ).astype(jnp.bfloat16)
    grad_gate = lax.dot_general(
        normed, d_gate, contract_first, preferred_element_type=jnp.float32
    ).astype(jnp.bfloat16)
    grad_up = lax.dot_general(
        normed, d_up, contract_first, preferred_element_type=jnp.float32
    ).astype(jnp.bfloat16)
    d_normed = lax.dot_general(d_gate, gate_w, contract_last, preferred_element_type=jnp.float32)
    d_normed = d_normed + lax.dot_general(
        d_up, up_w, contract_last, preferred_element_type=jnp.float32
    )
    pushed = norm_back(h_float, inv_rms, s_gain, d_normed)
    local_sum = jnp.sum(pushed.reshape(-1, length, width), axis=0) + own_cot.astype(jnp.float32)
    grad_total = lax.psum(local_sum.astype(jnp.bfloat16), "mem").astype(jnp.float32)
    cut_grad = (grad_total / lax.axis_size("mem")).astype(jnp.bfloat16)
    grad_q, grad_kv, grad_o = pull(cut_grad)
    summed = (
        lax.psum(grad_q.astype(jnp.float32).astype(jnp.bfloat16), "grp").astype(jnp.float32),
        lax.psum(grad_kv.astype(jnp.float32).astype(jnp.bfloat16), "grp").astype(jnp.float32),
        lax.psum(grad_o.astype(jnp.float32).astype(jnp.bfloat16), "grp").astype(jnp.float32),
    )
    groups = lax.axis_size("grp")
    grad_query = (summed[0] / groups).astype(jnp.bfloat16)
    grad_keyval = (summed[1] / groups).astype(jnp.bfloat16)
    grad_out = (summed[2] / groups).astype(jnp.bfloat16)
    return (
        server_out[None, None],
        grad_query[None],
        grad_keyval[None],
        grad_out[None],
        grad_gate[None],
        grad_up[None],
        grad_down[None],
    )


def solution(mesh):
    in_specs = (
        P("grp", "mem", None, None),
        P("mem", None),
        P("mem", None, None),
        P("mem", None, None),
        P("mem", None, None),
        P("grp", None),
        P("grp", None, "mem"),
        P("grp", None, "mem"),
        P("grp", "mem", None),
        P("grp", "mem", None, None),
        P("grp", "mem"),
    )
    out_specs = (
        P("grp", "mem", None, None),
        P("mem", None, None),
        P("mem", None, None),
        P("mem", None, None),
        P("grp", None, "mem"),
        P("grp", None, "mem"),
        P("grp", "mem", None),
    )
    return jax.shard_map(
        on_device, mesh=mesh, in_specs=in_specs, out_specs=out_specs, check_vma=False
    )
```

profile of v0, /device:TPU:0, one launch (start us, length us, event | category | flops | bytes accessed | tf_op | source)
XLA Modules:
  0.0 280.9 jit_solution(379847072400261066)
XLA Ops:
  9.6 11.2 %all_gather.7 = bf16[512,896]{1,0:T(8,128)(2,1)} all-gather(bf16[128,896]{1,0:T(8,128)(2,1)S(1)} %bitcast_select_fusion.1), channel_id=1, replica_groups=mesh['grp'=8,'mem'=4] {'mem'}, dimensions={0}, use_global_device_ids=true | all-gather | bytes 1146880 | tf_op jit(solution)/shard_map/all_gather | solution.py:77
  20.8 1.1 fusion.62
  23.7 1.9 fusion.37
  25.8 1.2 fusion.59
  30.4 9.9 %all_gather.6 = bf16[512,896]{1,0:T(8,128)(2,1)} all-gather(bf16[128,896]{1,0:T(8,128)(2,1)S(1)} %fusion.43), channel_id=1, replica_groups=mesh['grp'=8,'mem'=4] {'mem'}, dimensions={0}, use_global_device_ids=true | all-gather | bytes 1146880 | tf_op jit(solution)/shard_map/all_gather | solution.py:76
  40.3 1.3 reduce.1
  41.6 1.4 fusion.15
  43.0 3.5 %fusion.3 = f32[512,1216]{0,1:T(8,128)S(1)} fusion(bf16[512,896]{1,0:T(8,128)(2,1)} %all_gather.7, bf16[1,1216,896]{2,1,0:T(8,128)(2,1)} %param.19), kind=kOutput, calls=%fused_computation.16 | convolution fusion | flops 1115684864 | bytes 5586944 | tf_op jit(solution)/shard_map/dot_general | solution.py:93
  46.6 1.6 fusion.9
  48.2 3.7 %multiply_convert_fusion.3 = (bf16[512,1216]{0,1:T(8,128)(2,1)S(1)}, bf16[512,1216]{0,1:T(8,128)(2,1)}, bf16[512,1216]{0,1:T(8,128)(2,1)S(1)}) fusion(f32[512,1216]{0,1:T(8,128)S(1)} %fusion.3, f32[512,1216]{0,1:T(8,128)S(1)} %fusion.9, bf16[1,896,1216]{1,2,0:T(8,128)(2,1)S(1)} %copy-done, bf16[512,896]{1,0:T(8,128)(2,1)S(1)} %copy-done.1, ...), kind=kOutput, calls=%fused_computation.13 | convolution fusion | flops 1127481344 | bytes 11818496 | tf_op jit(solution)/shard_map/dot_general | solution.py:81
  51.9 1.5 fusion.7
  53.4 1.7 fusion.20
  55.2 1.6 fusion.19
  56.8 2.4 reduce_sum.84
  59.2 2.0 add_convert_fusion
  61.2 4.5 %fusion.31 = bf16[512,896]{1,0:T(8,128)(2,1)} fusion(bf16[512,1216]{0,1:T(8,128)(2,1)} %get-tuple-element.13, bf16[1,1216,896]{2,1,0:T(8,128)(2,1)} %param.19), kind=kOutput, calls=%fused_computation.45 | convolution fusion | flops 1116143616 | bytes 4341760 | tf_op jit(solution)/shard_map/dot_general | solution.py:86
  66.0 1.3 multiply_divide_fusion
  67.9 26.5 %all-reduce.6.cloned.1.call-done = bf16[128,896]{1,0:T(8,128)(2,1)} async-done(((bf16[128,896]{1,0:T(8,128)(2,1)}), bf16[128,896]{1,0:T(8,128)(2,1)}) %all-reduce.6.cloned.1.call-update) | async-done | bytes 229392 | tf_op jit(solution)/shard_map/psum | solution.py:111
  94.4 2.8 %fusion.40 = bf16[128,896]{1,0:T(8,128)(2,1)} fusion(bf16[1,896,896]{2,1,0:T(8,128)(2,1)} %param.15, bf16[128,896]{1,0:T(8,128)(2,1)} %all-reduce.6.cloned.1.call-done), kind=kOutput, calls=%fused_computation.54 | convolution fusion | flops 205979648 | bytes 2064384 | tf_op jit(solution)/shard_map/transpose(jvp())/dot_general | solution.py:32
  97.2 1.8 copy.31
  99.0 1.4 fusion.55
  102.1 1.2 convolution_convert_fusion.5
  103.5 1.7 convolution_convert_fusion.3
  105.2 1.8 convolution_convert_fusion.4
  107.1 4.5 %fusion = bf16[1,1216,896]{2,1,0:T(8,128)(2,1)} fusion(bf16[512,1216]{0,1:T(8,128)(2,1)} %get-tuple-element.13, bf16[512,896]{1,0:T(8,128)(2,1)} %all_gather.7), kind=kOutput, calls=%fused_computation.9 | convolution fusion | flops 1116774400 | bytes 4341760 | tf_op jit(solution)/shard_map/dot_general | solution.py:96
  111.7 2.9 %fusion.1 = bf16[1,896,1216]{1,2,0:T(8,128)(2,1)} fusion(bf16[512,1216]{0,1:T(8,128)(2,1)S(1)} %copy-done.36, bf16[512,896]{1,0:T(8,128)(2,1)S(1)} %copy-done.2, f32[896]{0:T(1024)S(1)} %copy-done.31, f32[512]{0:T(512)S(1)} %copy-done.27), kind=kOutput, calls=%fused_computation.10 | convolution fusion | flops 1118609408 | bytes 4347392 | tf_op jit(solution)/shard_map/dot_general | solution.py:99
  114.6 2.9 %fusion.2 = bf16[1,896,1216]{1,2,0:T(8,128)(2,1)} fusion(bf16[512,1216]{0,1:T(8,128)(2,1)S(1)} %copy-done.13, bf16[512,896]{1,0:T(8,128)(2,1)S(1)} %copy-done.2, f32[896]{0:T(1024)S(1)} %copy-done.31, f32[512]{0:T(512)S(1)} %copy-done.27), kind=kOutput, calls=%fused_computation.11 | convolution fusion | flops 1118609408 | bytes 4347392 | tf_op jit(solution)/shard_map/dot_general | solution.py:102
  117.5 3.5 %reduce-scatter.2.cloned.1.call-done = bf16[128,896]{1,0:T(8,128)(2,1)} async-done(((bf16[512,896]{1,0:T(8,128)(2,1)}), bf16[128,896]{1,0:T(8,128)(2,1)}) %reduce-scatter.2.cloned.1.call-update) | async-done | bytes 229392 | tf_op jit(solution)/shard_map/reduce_scatter | solution.py:85
  121.0 1.7 fusion.70
  122.7 145.6 %all-reduce.8.cloned.1.call-done = (bf16[896,896]{1,0:T(8,128)(2,1)}, bf16[896,256]{1,0:T(8,128)(2,1)}, bf16[896,896]{1,0:T(8,128)(2,1)}) async-done(((bf16[896,896]{1,0:T(8,128)(2,1)}, bf16[896,256]{1,0:T(8,128)(2,1)}, bf16[896,896]{1,0:T(8,128)(2,1)}), (bf16[896,896]{1,0:T(8,128)(2,1)}, bf16[896,256]{1,0:T(8,128)(2,1)}, bf16[896,896]{1,0:T(8,128)(2,1)})) %all-reduce.8.cloned.1.call-update) | async-done | bytes 3670032 | tf_op jit(solution)/shard_map/psum | solution.py:115
  268.3 1.9 fusion.67
  270.2 4.2 %fusion.21 = (bf16[1,896,896]{2,1,0:T(8,128)(2,1)}, bf16[1,896,896]{2,1,0:T(8,128)(2,1)}) fusion(bf16[896,896]{1,0:T(8,128)(2,1)} %get-tuple-element.9, bf16[896,896]{1,0:T(8,128)(2,1)} %get-tuple-element.11), kind=kLoop, calls=%fused_computation.37 | loop fusion | flops 4816896 | bytes 6422528 | tf_op jit(solution)/shard_map/broadcast_in_dim | solution.py:125
  (104 shorter events, 9.7 us)
Async XLA Ops:
  7.2 41.0 %copy-start = (bf16[1,896,1216]{1,2,0:T(8,128)(2,1)S(1)}, bf16[1,896,1216]{1,2,0:T(8,128)(2,1)}, u32[]{:S(2)}) copy-start(bf16[1,896,1216]{1,2,0:T(8,128)(2,1)} %param.17) | copy-start | bytes 6537220
  7.2 14.8 %copy-start.4 = (bf16[1,1,128,896]{3,2,1,0:T(8,128)(2,1)S(1)}, bf16[1,1,128,896]{3,2,1,0:T(8,128)(2,1)}, u32[]{:S(2)}) copy-start(bf16[1,1,128,896]{3,2,1,0:T(8,128)(2,1)} %param.11) | copy-start | bytes 688132
  7.2 14.7 %copy-start.32 = (f32[1,896]{1,0:T(1,128)S(1)}, f32[1,896]{1,0:T(1,128)}, u32[]{:S(2)}) copy-start(f32[1,896]{1,0:T(1,128)} %param.12) | copy-start | bytes 10756
  7.2 14.7 %copy-start.34 = (bf16[1,896,256]{2,1,0:T(8,128)(2,1)S(1)}, bf16[1,896,256]{2,1,0:T(8,128)(2,1)}, u32[]{:S(2)}) copy-start(bf16[1,896,256]{2,1,0:T(8,128)(2,1)} %param.14) | copy-start | bytes 1376260
  7.2 87.2 %all-reduce.6.cloned.1.call-start = ((), (), s32[]{:S(2)}) async-start(), calls=%async_computation.2 | async-start | bytes 458752 | tf_op jit(solution)/shard_map/psum | solution.py:111
  8.5 14.5 %copy-start.33 = (pred[128]{0:T(512)(128)(4,1)}, pred[128]{0:T(512)(128)(4,1)S(1)}, u32[]{:S(2)}) copy-start(pred[128]{0:T(512)(128)(4,1)S(1)} %iota_compare_fusion.2) | copy-start | bytes 388
  21.9 1.8 copy-start.28
  22.0 1.7 copy-start.24
  25.8 3.1 %copy-start.10 = (bf16[128,896]{0,1:T(8,128)(2,1)}, bf16[128,896]{0,1:T(8,128)(2,1)S(1)}, u32[]{:S(2)}) copy-start(bf16[128,896]{0,1:T(8,128)(2,1)S(1)} %copy.29) | copy-start | bytes 688132
  25.8 3.2 %copy-start.22 = (bf16[128,128]{0,1:T(8,128)(2,1)S(1)}, bf16[128,128]{0,1:T(8,128)(2,1)}, u32[]{:S(2)}) copy-start(bf16[128,128]{0,1:T(8,128)(2,1)} %copy.27) | copy-start | bytes 98308
  27.0 2.2 copy-start.18
  27.0 2.2 copy-start.3
  43.0 12.2 %copy-start.26 = (f32[512]{0:T(512)}, f32[512]{0:T(512)S(1)}, u32[]{:S(2)}) copy-start(f32[512]{0:T(512)S(1)} %get-tuple-element.20) | copy-start | bytes 6148
  43.0 3.6 %copy-start.1 = (bf16[512,896]{1,0:T(8,128)(2,1)S(1)}, bf16[512,896]{1,0:T(8,128)(2,1)}, u32[]{:S(2)}) copy-start(bf16[512,896]{1,0:T(8,128)(2,1)} %all_gather.6) | copy-start | bytes 2752516
  43.0 3.6 %copy-start.7 = (bf16[1,896,1216]{1,2,0:T(8,128)(2,1)S(1)}, bf16[1,896,1216]{1,2,0:T(8,128)(2,1)}, u32[]{:S(2)}) copy-start(bf16[1,896,1216]{1,2,0:T(8,128)(2,1)} %param.18) | copy-start | bytes 6537220
  43.0 3.6 %copy-start.30 = (f32[896]{0:T(1024)S(1)}, f32[896]{0:T(1024)}, u32[]{:S(2)}) copy-start(f32[896]{0:T(1024)} %reduce.1) | copy-start | bytes 10756
  51.9 1.5 copy-start.12
  51.9 1.6 copy-start.35
  61.2 59.8 %reduce-scatter.2.cloned.1.call-start = ((), (), s32[]{:S(2)}) async-start(), calls=%async_computation.1 | async-start | bytes 1146880 | tf_op jit(solution)/shard_map/reduce_scatter | solution.py:85
  65.8 202.6 %all-reduce.8.cloned.1.call-start = ((), (), s32[]{:S(2)}) async-start(), calls=%async_computation.3 | async-start | bytes 7340032 | tf_op jit(solution)/shard_map/psum | solution.py:115
  99.0 1.5 copy-start.16
  99.0 1.5 copy-start.19
  99.0 1.5 copy-start.21
  99.0 2.0 copy-start.23
  101.0 2.3 copy-start.17
  101.5 2.0 copy-start.15
  107.1 4.5 %copy-start.2 = (bf16[512,896]{1,0:T(8,128)(2,1)S(1)}, bf16[512,896]{1,0:T(8,128)(2,1)}, u32[]{:S(2)}) copy-start(bf16[512,896]{1,0:T(8,128)(2,1)} %all_gather.6) | copy-start | bytes 2752516
  107.1 4.5 %copy-start.27 = (f32[512]{0:T(512)S(1)}, f32[512]{0:T(512)}, u32[]{:S(2)}) copy-start(f32[512]{0:T(512)} %copy-done.26) | copy-start | bytes 6148
  107.1 4.5 %copy-start.31 = (f32[896]{0:T(1024)S(1)}, f32[896]{0:T(1024)}, u32[]{:S(2)}) copy-start(f32[896]{0:T(1024)} %reduce.1) | copy-start | bytes 10756
  107.1 4.5 %copy-start.36 = (bf16[512,1216]{0,1:T(8,128)(2,1)S(1)}, bf16[512,1216]{0,1:T(8,128)(2,1)}, u32[]{:S(2)}) copy-start(bf16[512,1216]{0,1:T(8,128)(2,1)} %copy-done.35) | copy-start | bytes 3735556
  111.7 2.9 %copy-start.13 = (bf16[512,1216]{0,1:T(8,128)(2,1)S(1)}, bf16[512,1216]{0,1:T(8,128)(2,1)}, u32[]{:S(2)}) copy-start(bf16[512,1216]{0,1:T(8,128)(2,1)} %copy-done.12) | copy-start | bytes 3735556
  114.6 6.4 %copy-start.9 = (bf16[128,896]{1,0:T(8,128)(2,1)S(1)}, bf16[128,896]{1,0:T(8,128)(2,1)}, u32[]{:S(2)}) copy-start(bf16[128,896]{1,0:T(8,128)(2,1)} %copy-done.8) | copy-start | bytes 688132
  (8 other events, 8.5 us)
Sparse Core Ops, SparseCore 0:
  61.3 33.0 all-reduce.5
  96.9 24.0 reduce-scatter.1
  125.5 142.7 all-reduce.7
where the time goes:
time: 282 us; the launch traced here: 281 us
  waiting for transfers between devices  176 us (62%)
  matrix products  40.7 us (14%)
  other arithmetic  23.9 us (8%)
  blocking collectives  21.1 us (7%)
  between operations  15 us (5%)
  local copies, waits for them, and re-layouts  4.24 us (2%)
    psum x1, waiting for transfers between devices, on_device(): lax.psum(grad_q.astype(jnp.float32).astype(jnp.bfloat16), 'grp')  146 us
    psum x1, waiting for transfers between devices, on_device(): lax.psum(local_sum.astype(jnp.bfloat16), 'mem').astype(jnp.float32)  26.5 us
    all_gather x1, blocking collectives, on_device(): all_cot = lax.all_gather(own_cot, 'mem', axis=0, tiled=True)  11.2 us
    all_gather x1, blocking collectives, on_device(): all_cut = lax.all_gather(own_cut, 'mem', axis=0, tiled=True)  9.85 us
  transfers between devices with their start and end apart: 3, of which 3 were waited for; matrix products, arithmetic and copies ran while one was open for 11% of the time, Pallas kernels for 0%

commit v1 on v0

--- a/solution.py
+++ b/solution.py
@@ -6,6 +6,7 @@
 KV_HEADS = 2
 HEAD_DIM = 64
 EPS = 1e-06
+supply_clusters_for = lambda arr, link_axis: jnp.sum(lax.all_gather(arr, axis_name=link_axis), 0)
 
 
 def client_forward(tokens_in, gain_vec, query_w, keyval_w, output_w):
@@ -112,7 +113,9 @@
     cut_grad = (grad_total / lax.axis_size("mem")).astype(jnp.bfloat16)
     grad_q, grad_kv, grad_o = pull(cut_grad)
     summed = (
-        lax.psum(grad_q.astype(jnp.float32).astype(jnp.bfloat16), "grp").astype(jnp.float32),
+        supply_clusters_for(grad_q.astype(jnp.float32).astype(jnp.bfloat16), "grp").astype(
+            jnp.float32
+        ),
         lax.psum(grad_kv.astype(jnp.float32).astype(jnp.bfloat16), "grp").astype(jnp.float32),
         lax.psum(grad_o.astype(jnp.float32).astype(jnp.bfloat16), "grp").astype(jnp.float32),
     )

time: 282 us -> 426 us (1.51)
  waiting for transfers between devices: 176 us -> 309 us
  other arithmetic: 23.9 us -> 33.5 us
    all_gather x0 -> x1, waiting for transfers between devices: none -> 177 us  [lax.all_gather(arr, axis_name=link_axis)]
    psum x1, waiting for transfers between devices: 146 us -> 104 us  [on_device(): lax.psum(grad_kv.astype(jnp.float32).astype(jnp.bfloat16), 'grp')]
    reduce_sum x0 -> x1, other arithmetic: none -> 8.02 us  [jnp.sum(lax.all_gather(arr, axis_name=link_axis), 0)]
  transfers between devices with their start and end apart: 3 -> 4, of which waited for: 3 -> 4; matrix products, arithmetic and copies ran while one was open for 11% -> 8% of each run, Pallas kernels for 0% -> 0%
where the time goes in v1:
time: 426 us; the launch traced here: 425 us
  waiting for transfers between devices  309 us (73%)
  matrix products  40.7 us (10%)
  other arithmetic  33.5 us (8%)
  blocking collectives  21.1 us (5%)
  between operations  15 us (4%)
  local copies, waits for them, and re-layouts  5.39 us (1%)
    all_gather x1, waiting for transfers between devices, lax.all_gather(arr, axis_name=link_axis)  177 us
    psum x1, waiting for transfers between devices, on_device(): lax.psum(grad_kv.astype(jnp.float32).astype(jnp.bfloat16), 'grp')  104 us
    psum x1, waiting for transfers between devices, on_device(): lax.psum(local_sum.astype(jnp.bfloat16), 'mem').astype(jnp.float32)  26.5 us
    all_gather x1, blocking collectives, on_device(): all_cot = lax.all_gather(own_cot, 'mem', axis=0, tiled=True)  11.2 us
    all_gather x1, blocking collectives, on_device(): all_cut = lax.all_gather(own_cut, 'mem', axis=0, tiled=True)  9.85 us
  transfers between devices with their start and end apart: 4, of which 4 were waited for; matrix products, arithmetic and copies ran while one was open for 8% of the time, Pallas kernels for 0%

profile of v1, /device:TPU:0, one launch (start us, length us, event | category | flops | bytes accessed | tf_op | source)
XLA Modules:
  0.0 425.2 jit_solution(13079722995035683592)
XLA Ops:
  9.6 11.2 %all_gather.13 = bf16[512,896]{1,0:T(8,128)(2,1)} all-gather(bf16[128,896]{1,0:T(8,128)(2,1)S(1)} %bitcast_select_fusion.1), channel_id=1, replica_groups=mesh['grp'=8,'mem'=4] {'mem'}, dimensions={0}, use_global_device_ids=true | all-gather | bytes 1146880 | tf_op jit(solution)/shard_map/all_gather | solution.py:78
  23.7 1.9 fusion.37
  30.4 9.9 %all_gather.12 = bf16[512,896]{1,0:T(8,128)(2,1)} all-gather(bf16[128,896]{1,0:T(8,128)(2,1)S(1)} %fusion.43), channel_id=1, replica_groups=mesh['grp'=8,'mem'=4] {'mem'}, dimensions={0}, use_global_device_ids=true | all-gather | bytes 1146880 | tf_op jit(solution)/shard_map/all_gather | solution.py:77
  40.3 1.3 reduce.2
  41.6 1.4 fusion.15
  43.1 3.5 fusion.3
  46.6 1.6 fusion.9
  48.2 3.7 multiply_convert_fusion.3
  51.9 1.5 fusion.7
  53.5 1.7 fusion.20
  55.2 1.6 fusion.19
  56.8 2.4 reduce_sum.96
  59.2 2.0 add_convert_fusion
  61.3 4.5 %fusion.31 = bf16[512,896]{1,0:T(8,128)(2,1)} fusion(bf16[512,1216]{0,1:T(8,128)(2,1)} %get-tuple-element.12, bf16[1,1216,896]{2,1,0:T(8,128)(2,1)} %param.19), kind=kOutput, calls=%fused_computation.45 | convolution fusion | flops 1116143616 | bytes 4341760 | tf_op jit(solution)/shard_map/dot_general | solution.py:87
  66.0 1.3 multiply_divide_fusion
  67.9 26.5 %all-reduce.6.cloned.1.call-done = bf16[128,896]{1,0:T(8,128)(2,1)} async-done(((bf16[128,896]{1,0:T(8,128)(2,1)}), bf16[128,896]{1,0:T(8,128)(2,1)}) %all-reduce.6.cloned.1.call-update) | async-done | bytes 229392 | tf_op jit(solution)/shard_map/psum | solution.py:112
  94.4 2.8 fusion.40
  97.2 1.8 copy.31
  99.0 1.4 fusion.55
  104.1 1.7 convolution_convert_fusion.3
  106.5 1.8 convolution_convert_fusion.4
  108.4 4.5 %fusion = bf16[1,1216,896]{2,1,0:T(8,128)(2,1)} fusion(bf16[512,1216]{0,1:T(8,128)(2,1)} %get-tuple-element.12, bf16[512,896]{1,0:T(8,128)(2,1)} %all_gather.13), kind=kOutput, calls=%fused_computation.9 | convolution fusion | flops 1116774400 | bytes 4341760 | tf_op jit(solution)/shard_map/dot_general | solution.py:97
  112.9 2.9 fusion.1
  115.9 2.9 fusion.2
  118.8 2.2 reduce-scatter.2.cloned.1.call-done
  121.0 1.7 fusion.70
  122.7 103.8 %all-reduce.8.cloned.1.call-done = (bf16[896,256]{1,0:T(8,128)(2,1)}, bf16[896,896]{1,0:T(8,128)(2,1)}) async-done(((bf16[896,256]{1,0:T(8,128)(2,1)}, bf16[896,896]{1,0:T(8,128)(2,1)}), (bf16[896,256]{1,0:T(8,128)(2,1)}, bf16[896,896]{1,0:T(8,128)(2,1)})) %all-reduce.8.cloned.1.call-update) | async-done | bytes 2064400 | tf_op jit(solution)/shard_map/psum | solution.py:119
  226.5 1.9 fusion.67
  228.4 2.9 fusion.22
  231.3 176.5 %all-gather.3.cloned.1.call-done = bf16[7168,896]{1,0:T(8,128)(2,1)} async-done(((bf16[896,896]{1,0:T(8,128)(2,1)}), bf16[7168,896]{1,0:T(8,128)(2,1)}) %all-gather.3.cloned.1.call-update) | async-done | bytes 12845072 | tf_op jit(solution)/shard_map/all_gather | solution.py:9
  407.8 8.0 %reduce_sum.100 = bf16[896,896]{1,0:T(8,128)(2,1)} reduce(bf16[8,896,896]{2,1,0:T(8,128)(2,1)} %bitcast.179, bf16[]{:T(256)} %constant.33.clone.1), dimensions={0}, to_apply=%region_11.12 | reduce | flops 5619712 | bytes 14450690 | tf_op jit(solution)/shard_map/reduce_sum | solution.py:9
  415.8 2.9 fusion.21
  (117 shorter events, 14.3 us)
Async XLA Ops:
  7.2 41.0 %copy-start = (bf16[1,896,1216]{1,2,0:T(8,128)(2,1)S(1)}, bf16[1,896,1216]{1,2,0:T(8,128)(2,1)}, u32[]{:S(2)}) copy-start(bf16[1,896,1216]{1,2,0:T(8,128)(2,1)} %param.17) | copy-start | bytes 6537220
  7.2 14.8 %copy-start.4 = (bf16[1,1,128,896]{3,2,1,0:T(8,128)(2,1)S(1)}, bf16[1,1,128,896]{3,2,1,0:T(8,128)(2,1)}, u32[]{:S(2)}) copy-start(bf16[1,1,128,896]{3,2,1,0:T(8,128)(2,1)} %param.11) | copy-start | bytes 688132
  7.2 14.7 %copy-start.36 = (f32[1,896]{1,0:T(1,128)S(1)}, f32[1,896]{1,0:T(1,128)}, u32[]{:S(2)}) copy-start(f32[1,896]{1,0:T(1,128)} %param.12) | copy-start | bytes 10756
  7.2 14.8 %copy-start.38 = (bf16[1,896,256]{2,1,0:T(8,128)(2,1)S(1)}, bf16[1,896,256]{2,1,0:T(8,128)(2,1)}, u32[]{:S(2)}) copy-start(bf16[1,896,256]{2,1,0:T(8,128)(2,1)} %param.14) | copy-start | bytes 1376260
  7.2 87.2 %all-reduce.6.cloned.1.call-start = ((), (), s32[]{:S(2)}) async-start(), calls=%async_computation.2 | async-start | bytes 458752 | tf_op jit(solution)/shard_map/psum | solution.py:112
  8.5 13.4 %copy-start.37 = (pred[128]{0:T(512)(128)(4,1)}, pred[128]{0:T(512)(128)(4,1)S(1)}, u32[]{:S(2)}) copy-start(pred[128]{0:T(512)(128)(4,1)S(1)} %iota_compare_fusion.2) | copy-start | bytes 388
  21.9 3.9 copy-start.31
  22.0 3.9 copy-start.26
  25.8 3.1 copy-start.12
  25.8 3.2 copy-start.24
  27.0 2.2 copy-start.20
  27.0 2.2 copy-start.3
  43.0 12.2 %copy-start.29 = (f32[512]{0:T(512)}, f32[512]{0:T(512)S(1)}, u32[]{:S(2)}) copy-start(f32[512]{0:T(512)S(1)} %get-tuple-element.19) | copy-start | bytes 6148
  43.0 3.6 copy-start.1
  43.0 3.6 copy-start.9
  43.0 3.6 copy-start.34
  61.2 59.8 %reduce-scatter.2.cloned.1.call-start = ((), (), s32[]{:S(2)}) async-start(), calls=%async_computation.1 | async-start | bytes 1146880 | tf_op jit(solution)/shard_map/reduce_scatter | solution.py:86
  65.8 160.7 %all-reduce.8.cloned.1.call-start = ((), (), s32[]{:S(2)}) async-start(), calls=%async_computation.4 | async-start | bytes 4128768 | tf_op jit(solution)/shard_map/psum | solution.py:119
  99.0 2.0 copy-start.25
  100.5 2.0 copy-start.8
  100.5 2.0 copy-start.16
  101.0 1.9 copy-start.27
  101.0 1.9 copy-start.32
  101.0 3.1 copy-start.17
  104.1 1.8 copy-start.19
  105.8 302.0 %all-gather.3.cloned.1.call-start = ((), (), s32[]{:S(2)}) async-start(), calls=%async_computation.3 | async-start | bytes 14450688 | tf_op jit(solution)/shard_map/all_gather | solution.py:9
  108.4 4.5 %copy-start.2 = (bf16[512,896]{1,0:T(8,128)(2,1)S(1)}, bf16[512,896]{1,0:T(8,128)(2,1)}, u32[]{:S(2)}) copy-start(bf16[512,896]{1,0:T(8,128)(2,1)} %all_gather.12) | copy-start | bytes 2752516
  108.4 4.5 %copy-start.30 = (f32[512]{0:T(512)S(1)}, f32[512]{0:T(512)}, u32[]{:S(2)}) copy-start(f32[512]{0:T(512)} %copy-done.29) | copy-start | bytes 6148
  108.4 4.5 %copy-start.35 = (f32[896]{0:T(1024)S(1)}, f32[896]{0:T(1024)}, u32[]{:S(2)}) copy-start(f32[896]{0:T(1024)} %reduce.2) | copy-start | bytes 10756
  108.4 4.5 %copy-start.40 = (bf16[512,1216]{0,1:T(8,128)(2,1)S(1)}, bf16[512,1216]{0,1:T(8,128)(2,1)}, u32[]{:S(2)}) copy-start(bf16[512,1216]{0,1:T(8,128)(2,1)} %copy-done.39) | copy-start | bytes 3735556
  112.9 2.9 copy-start.15
  115.9 5.2 %copy-start.11 = (bf16[128,896]{1,0:T(8,128)(2,1)S(1)}, bf16[128,896]{1,0:T(8,128)(2,1)}, u32[]{:S(2)}) copy-start(bf16[128,896]{1,0:T(8,128)(2,1)} %copy-done.10) | copy-start | bytes 688132
  (13 other events, 15.9 us)
Sparse Core Ops, SparseCore 0:
  61.3 33.0 all-reduce.5
  97.0 24.0 reduce-scatter.1
  125.3 101.1 all-reduce.7
  229.2 178.6 all-gather.2
